TPU v7x, 256 devices: a whole 4x4x8 slice. The times are simulated.
256 devices in a mesh: band: 64 (over x, z, core), dir: 4 (over y).
Axes of the slice: x: 4, y: 4, z: 8, core: 2. Of those that a mesh axis runs over, the one named last changes fastest.
Arguments:
- visibilities: bfloat16 [128, 32, 2, 256, 256], P('band', 'dir'), as said below
- sky_model: bfloat16 [128, 32, 2, 256, 256], P('band', 'dir')
- rfi_flags: int32 [128, 8, 8], P('band'), may hold values from 0 to 1, as said below
- destination: int32 [128], P('band'), may hold values from 0 to 127, as said below
Outputs:
- delivered: float32 [128, 32, 2, 256], P('band', 'dir')
- coefficients: float32 [9, 32, 2, 256], P(None, 'dir')
- norm_values: float32 [2, 2], replicated
Inputs may be any that keep to these rules, and one draw needn't show every extreme that they name: `rfi_flags`: 1 marks a flagged baseline block; the share of flagged blocks tends to fall with the subband index. destination holds every row of 0 to 127 once. With the rows split into 64 aligned blocks of 2 rows, one row of block i goes to a row of block i + 1 and the other to a row of block i + 32, modulo 128 // 2. `visibilities`: visibilities follow the model under unknown station gains, with noise.
All inputs are finite; a program needn't handle non-finite values.
Results may differ from a plain program's by a relative error of at most 0.0003.
Values sent between devices are 32-bit elements; how exact they have to be, the bound alone decides.
A program may use at most 128 MiB of HBM per device.

v0:
```python
import jax
import jax.numpy as jnp
from jax import lax
from jax.experimental import pallas as pl
from jax.experimental.pallas import tpu as pltpu
from jax.sharding import PartitionSpec as P

DEGREE = 8
SWEEPS = 4
TERMS = DEGREE + 1
BANDS = 64
OWNERS = 32
DIRS = 4
ROWS = 16
HALF = 128

f32 = jnp.float32
bf16 = jnp.bfloat16
HIGHEST = lax.Precision.HIGHEST
MESH = pl.DeviceIdType.MESH
penalty_share = 0.4


def iota(shape, dim):
    return lax.broadcasted_iota(jnp.int32, shape, dim)


def gather(x, index, axis):
    return jnp.take_along_axis(x, index, axis=axis, mode="promise_in_bounds")


def dot(a, b, contract):
    return lax.dot_general(
        a, b, (contract, ((), ())), precision=HIGHEST, preferred_element_type=f32
    )


def kernel(
    flags, dest, vis, sky, dlv_out, coef_out, norm_out,
    visb, skyb, are, aim, bsq, tre, tim, tmag, num, row, tgt, pens,
    wsend, wrecv, asend, arecv, bsend, brecv, csend, crecv, near_s, far_s, near_r, far_r,
    dsend, drecv, esend, erecv, proj, spread, norm0, dummy,
    in_sem, w_ss, w_rs, a_ss, a_rs, b_ss, b_rs, c_ss, c_rs, n_ss, n_rs, f_ss, f_rs,
    d_ss, d_rs, e_ss, e_rs,
):
    me = lax.axis_index("band")
    plane = lax.axis_index("dir")
    chip = me // 2
    core = lax.rem(me, 2)

    def copy_to(src, dst, ss, rs, target):
        return pltpu.make_async_remote_copy(
            src_ref=src, dst_ref=dst, send_sem=ss, recv_sem=rs,
            device_id={"band": target}, device_id_type=MESH,
        )

    def chunk(i, arr, buf, s):
        f, c = i // 4, lax.rem(i, 4)
        rows = pl.ds(pl.multiple_of(c * 64, 64), 64)
        return pltpu.make_async_copy(
            arr.at[f, :, :, rows, :], buf.at[f, :, :, rows, :], in_sem.at[s, i]
        )

    for i in range(8):
        chunk(i, vis, visb, 0).start()
        chunk(i, sky, skyb, 1).start()

    barrier = pltpu.get_barrier_semaphore()

    def greet(t, _):
        pl.semaphore_signal(
            barrier, inc=1, device_id={"band": lax.rem(me + t, BANDS)}, device_id_type=MESH
        )
        return 0

    lax.fori_loop(1, BANDS, greet, 0)
    for t in range(1, DIRS):
        pl.semaphore_signal(
            barrier, inc=1, device_id={"dir": lax.rem(plane + t, DIRS)}, device_id_type=MESH
        )

    for f in range(2):
        count = jnp.int32(0)
        for a in range(8):
            for b in range(8):
                count = count + (1 - flags[f, a, b])
        weight = (1.0 + jnp.full((8, HALF), count, jnp.int32).astype(f32)) / 65.0
        pens[f] = penalty_share * 256.0 * weight
        wsend[pl.ds(f, 1), :] = weight[0:1, :]

    lane16 = lax.rem(iota((8, HALF), 1), 16)
    group = iota((8, HALF), 1) // 16
    sub = iota((8, HALF), 0)
    spread_index = [group * 16 + half * 8 + sub for half in range(2)]
    mix1 = lax.rem(group + sub, 8) * 16 + lane16
    mix2 = lax.rem(sub - group + 8, 8)
    mix3 = lax.rem(sub - group + 8, 8) * 16 + lane16

    def swap_groups(x):
        return gather(gather(gather(x, mix1, 1), mix2, 0), mix3, 1)

    q_lane = iota((ROWS, HALF), 1)
    p_sub = iota((ROWS, HALF), 0)

    def operator_block(t, _):
        f, ph = t // ROWS, lax.rem(t, ROWS)

        @pl.when(lax.rem(ph, 4) == 0)
        def _():
            i = t // 4
            chunk(i, vis, visb, 0).wait()
            chunk(i, sky, skyb, 1).wait()

        rows = pl.ds(pl.multiple_of(ph * ROWS, ROWS), ROWS)
        sums = []
        for qh in range(2):
            keep = [
                jnp.full((ROWS, HALF), 1 - flags[f, ph // 2, qh * 4 + b], jnp.int32)
                for b in range(4)
            ]
            kept = keep[3]
            for b in (2, 1, 0):
                kept = jnp.where(q_lane < (b + 1) * 32, keep[b], kept)
            apart = q_lane + qh * HALF != p_sub + ph * ROWS
            mask = jnp.where(apart, kept, 0).astype(f32).astype(bf16)[None]
            lanes = pl.ds(qh * HALF, HALF)

            def flipped(x):
                return x.reshape(HALF, HALF).T.astype(f32)

            mr = flipped(skyb[f, :, 0, rows, lanes] * mask)
            mi = flipped(skyb[f, :, 1, rows, lanes] * mask)
            dr = flipped(visb[f, :, 0, rows, lanes])
            di = flipped(visb[f, :, 1, rows, lanes])
            ar = mr * dr + mi * di
            ai = mr * di - mi * dr
            b2 = mr * mr + mi * mi
            are[f, ph, pl.ds(qh * HALF, HALF), :] = ar
            aim[f, ph, pl.ds(qh * HALF, HALF), :] = ai
            bsq[f, ph, pl.ds(qh * HALF, HALF), :] = b2
            sums.append([jnp.sum(v, axis=0, keepdims=True) for v in (ar, ai, b2)])
        for n in range(3):
            num[f, n, pl.ds(ph, 1), :] = sums[0][n] + sums[1][n]
        return 0

    lax.fori_loop(0, 2 * ROWS, operator_block, 0)

    pl.semaphore_wait(barrier, BANDS - 1 + DIRS - 1)

    def to_owners(src_of, dst, ss, rs):
        def send(t, _):
            j = lax.rem(chip + t, OWNERS)
            copy_to(src_of(j), dst.at[me], ss, rs, 2 * j + 1).start()
            return 0

        lax.fori_loop(1, OWNERS, send, 0)

        @pl.when(core == 0)
        def _():
            copy_to(src_of(chip), dst.at[me], ss, rs, me + 1).start()

    to_owners(lambda j: wsend, wrecv, w_ss, w_rs)

    @pl.when(core == 1)
    def _():
        wrecv[me] = wsend[...]

    ones = jnp.ones((ROWS, HALF), f32)
    zeros = jnp.zeros((ROWS, HALF), f32)
    for f in range(2):
        row[f, 0] = ones
        row[f, 1] = zeros
        tgt[f, 0] = ones
        tgt[f, 1] = zeros

    def update(f, odd):
        pen = jnp.concatenate([pens[f], pens[f]], axis=0)
        below = num[f, 2] + pen
        new = []
        for part in range(2):
            fresh = (num[f, part] + pen * tgt[f, part]) / below
            fresh = jnp.where(odd, 0.5 * (fresh + row[f, part]), fresh)
            row[f, part] = fresh
            new.append(fresh)
        return new

    def tiles(f, new):
        for ph in range(ROWS):
            for half in range(2):
                at = pl.ds(ph * ROWS + half * 8, 8)
                t = [
                    gather(
                        jnp.broadcast_to(v[ph : ph + 1, :], (8, HALF)), spread_index[half], 1
                    )
                    for v in new
                ]
                tre[f, at, :] = t[0]
                tim[f, at, :] = t[1]
                tmag[f, at, :] = t[0] * t[0] + t[1] * t[1]

    GROUP = 4

    def matvec(f):
        def block(pb, _):
            acc = [[jnp.zeros((8, HALF), f32) for _ in range(3)] for _ in range(GROUP)]
            for q in range(32):
                at = pl.ds(q * 8, 8)
                gr, gi, gm = tre[f, at, :], tim[f, at, :], tmag[f, at, :]
                for j in range(GROUP):
                    ph = pb * GROUP + j
                    a, b = are[f, ph, at, :], aim[f, ph, at, :]
                    acc[j][0] = acc[j][0] + (a * gr - b * gi)
                    acc[j][1] = acc[j][1] + (a * gi + b * gr)
                    acc[j][2] = acc[j][2] + bsq[f, ph, at, :] * gm
            for j in range(GROUP):
                for n in range(3):
                    num[f, n, pl.ds(pb * GROUP + j, 1), :] = jnp.sum(
                        acc[j][n], axis=0, keepdims=True
                    )
            return 0

        lax.fori_loop(0, ROWS // GROUP, block, 0)

    def sweep(s, f):
        matvec(f)
        tiles(f, update(f, lax.rem(s, 2) == 1))
        return 0

    for f in range(2):
        tiles(f, update(f, False))

    def sweeps(t, _):
        return sweep(t // 2, lax.rem(t, 2))

    lax.fori_loop(2, 2 * SWEEPS, sweeps, 0)

    def natural(f):
        return [
            [swap_groups(row[f, part, h * 8 : h * 8 + 8, :]) for h in range(2)]
            for part in range(2)
        ]

    def pack(dst):
        for f in range(2):
            n = natural(f)
            for part in range(2):
                for h in range(2):
                    dst[pl.ds((part * 2 + h) * 8, 8), f, :] = n[part][h]

    pack(asend)
    to_owners(lambda j: asend.at[j], arecv, a_ss, a_rs)

    def both(ref):
        return jnp.concatenate([ref[:, 0, :], ref[:, 1, :]], axis=0)

    def await_bytes(ref, ss, rs, sent):
        c = copy_to(ref, ref, ss, rs, lax.rem(me + 1, BANDS))
        c.wait_send() if sent else c.wait_recv()

    @pl.when(core == 1)
    def _():
        arecv[me] = asend[chip]
        await_bytes(wrecv.at[pl.ds(0, BANDS - 1)], w_ss, w_rs, False)
        weight = both(wrecv)
        r = iota((HALF, HALF), 0)
        lane = iota((HALF, HALF), 1)
        band_row = (lax.rem(r, BANDS) * 2 + r // BANDS).astype(f32)
        x = (2.0 * band_row + 1.0) / 128.0 - 1.0
        basis = jnp.where(lane == 0, 1.0, jnp.where(lane == 1, x, 0.0))
        before, now = jnp.ones_like(x), x
        for c in range(2, TERMS):
            before, now = now, 2.0 * x * now - before
            basis = jnp.where(lane == c, now, basis)
        weighted = basis * weight
        gram = dot(weighted, basis, ((0,), (0,)))[:ROWS, :]
        r16, l16 = iota((ROWS, HALF), 0), iota((ROWS, HALF), 1)
        m = jnp.where((r16 >= TERMS) & (l16 == r16), 1.0, gram)
        m = jnp.where(l16 == r16 + 16, 1.0, m)
        for c in range(TERMS):
            line = m[c : c + 1, :] / m[c : c + 1, c : c + 1]
            m = jnp.where(r16 == c, line, m - m[:, c : c + 1] * line)
        inverse = m[:, 16:32]
        proj[...] = dot(inverse, weighted[:, :ROWS], ((1,), (1,)))
        spread[...] = dot(basis[:, :ROWS], proj[...], ((1,), (0,)))
        scale = 1.0 / (16384.0 * jnp.sum(weight, axis=0, keepdims=True))

        await_bytes(arecv.at[pl.ds(0, BANDS - 1)], a_ss, a_rs, False)
        gain = both(arecv)
        fresh = dot(spread[...], gain, ((1,), (0,)))
        bsend[:, 0, :] = fresh[:BANDS, :]
        bsend[:, 1, :] = fresh[BANDS:, :]

        def back(t, _):
            i = lax.rem(me + t, BANDS)
            copy_to(bsend.at[i], brecv.at[chip], b_ss, b_rs, i).start()
            return 0

        lax.fori_loop(1, BANDS, back, 0)
        brecv[chip] = bsend[me]
        first = jnp.where(chip < 16, 1.0, 0.0)
        norm0[0:1, :] = scale * jnp.sum(weight * (gain - fresh) ** 2, axis=0, keepdims=True)
        norm0[1:2, :] = scale * jnp.sum(weight * (fresh - first) ** 2, axis=0, keepdims=True)
        norm0[2:3, :] = scale
        await_bytes(brecv.at[pl.ds(0, OWNERS - 1)], b_ss, b_rs, False)

    @pl.when(core == 0)
    def _():
        await_bytes(brecv, b_ss, b_rs, False)

    for f in range(2):
        for part in range(2):
            for h in range(2):
                lines = brecv[pl.ds((part * 2 + h) * 8, 8), f, :]
                at = slice(h * 8, h * 8 + 8)
                tgt[f, part, at, :] = 2.0 * swap_groups(lines) - row[f, part, at, :]

    lax.fori_loop(0, 2 * SWEEPS, sweeps, 0)

    pack(csend)
    to_owners(lambda j: csend.at[j], crecv, c_ss, c_rs)

    near = lax.rem(me + 1, BANDS)
    far = lax.rem(me + BANDS // 2, BANDS)
    first_near = jnp.full((OWNERS, HALF), dest[0] // 2, jnp.int32) == near
    row_a, row_b = csend[:, 0, :], csend[:, 1, :]
    near_rows = jnp.where(first_near, row_a, row_b)
    far_rows = jnp.where(first_near, row_b, row_a)
    near_s[pl.ds(0, OWNERS), 0, :] = near_rows
    far_s[...] = far_rows.reshape(OWNERS, 1, HALF)
    slots = [jnp.full((1, HALF), lax.rem(dest[f], 2), jnp.int32).astype(f32) for f in range(2)]
    near_s[pl.ds(OWNERS, 1), 0, :] = jnp.where(first_near[:1], slots[0], slots[1])
    copy_to(near_s, near_r, n_ss, n_rs, near).start()
    copy_to(far_s, far_r, f_ss, f_rs, far).start()

    @pl.when(core == 1)
    def _():
        crecv[me] = csend[chip]
        gain0 = both(arecv)
        fresh0 = both(bsend)
        weight = both(wrecv)
        scale = norm0[2:3, :]
        await_bytes(crecv.at[pl.ds(0, BANDS - 1)], c_ss, c_rs, False)
        gain = both(crecv)
        moved = gain + (gain0 - fresh0)
        coef = dot(proj[...], moved, ((1,), (0,)))
        fresh = dot(spread[...], moved, ((1,), (0,)))
        primal = scale * jnp.sum(weight * (gain - fresh) ** 2, axis=0, keepdims=True)
        dual = scale * jnp.sum(weight * (fresh - fresh0) ** 2, axis=0, keepdims=True)
        lane = iota((1, HALF), 1)
        line = jnp.zeros((1, HALF), f32)
        for n, v in enumerate((norm0[0:1, :], norm0[1:2, :], primal, dual)):
            line = jnp.where(lane == n, jnp.sum(v, axis=1, keepdims=True), line)
        for k in range(5):
            dsend[k] = coef[2 * k : 2 * k + 2, :]
        dsend[4, pl.ds(1, 1), :] = line

        def spread_out(t, _):
            i = lax.rem(me + t, BANDS)
            copy_to(dsend, drecv.at[chip], d_ss, d_rs, i).start()
            return 0

        lax.fori_loop(1, BANDS, spread_out, 0)
        drecv[chip] = dsend[...]

    await_bytes(near_r, n_ss, n_rs, False)
    await_bytes(far_r, f_ss, f_rs, False)
    slot = near_r[OWNERS, 0:1, :]
    for part in range(2):
        for h in range(2):
            at = pl.ds((part * 2 + h) * 8, 8)
            a, b = near_r[at, 0, :], far_r[at, 0, :]
            swap = jnp.broadcast_to(slot, (8, HALF)) > 0.5
            lanes = pl.ds(h * HALF, HALF)
            dlv_out[0, :, part, lanes] = jnp.where(swap, b, a)
            dlv_out[1, :, part, lanes] = jnp.where(swap, a, b)

    @pl.when(core == 1)
    def _():
        await_bytes(drecv.at[pl.ds(0, OWNERS - 1)], d_ss, d_rs, False)

    @pl.when(core == 0)
    def _():
        await_bytes(drecv, d_ss, d_rs, False)

    esend[...] = jnp.sum(drecv[:, 4, 1, :], axis=0, keepdims=True)
    for t in range(1, DIRS):
        pltpu.make_async_remote_copy(
            src_ref=esend, dst_ref=erecv.at[t - 1], send_sem=e_ss, recv_sem=e_rs.at[t - 1],
            device_id={"dir": lax.rem(plane + t, DIRS)}, device_id_type=MESH,
        ).start()
    for c in range(TERMS):
        for part in range(2):
            for h in range(2):
                at = pl.ds((part * 2 + h) * 8, 8)
                coef_out[c, :, part, pl.ds(h * HALF, HALF)] = drecv[at, c // 2, c % 2, :]
    total = esend[...]
    for t in range(1, DIRS):
        pltpu.make_async_remote_copy(
            src_ref=esend, dst_ref=erecv.at[t - 1], send_sem=e_ss, recv_sem=e_rs.at[t - 1],
            device_id={"dir": lax.rem(plane + t, DIRS)}, device_id_type=MESH,
        ).wait_recv()
    for t in range(1, DIRS):
        total = total + erecv[t - 1]
    norm_out[...] = jnp.sqrt(total)

    await_bytes(erecv, e_ss, e_rs.at[0], True)
    await_bytes(near_s, n_ss, n_rs, True)
    await_bytes(far_s, f_ss, f_rs, True)

    @pl.when(core == 1)
    def _():
        await_bytes(wrecv.at[pl.ds(0, OWNERS - 1)], w_ss, w_rs, True)
        await_bytes(asend.at[pl.ds(0, OWNERS - 1)], a_ss, a_rs, True)
        await_bytes(csend.at[pl.ds(0, OWNERS - 1)], c_ss, c_rs, True)
        await_bytes(bsend.at[pl.ds(0, BANDS - 1)], b_ss, b_rs, True)
        await_bytes(dummy, d_ss, d_rs, True)

    @pl.when(core == 0)
    def _():
        await_bytes(wrecv.at[pl.ds(0, OWNERS)], w_ss, w_rs, True)
        await_bytes(asend, a_ss, a_rs, True)
        await_bytes(csend, c_ss, c_rs, True)


def per_device(visibilities, sky_model, rfi_flags, destination):
    vmem = pltpu.VMEM
    dma = pltpu.SemaphoreType.DMA
    big = vmem((2, ROWS, 256, HALF), f32)
    tile = vmem((2, 256, HALF), f32)
    lines = vmem((OWNERS, 2, HALF), f32)
    every = vmem((BANDS, 2, HALF), f32)
    scratch = [
        vmem((2, 8, 2, 256, 256), bf16), vmem((2, 8, 2, 256, 256), bf16),
        big, big, big, tile, tile, tile,
        vmem((2, 3, ROWS, HALF), f32), vmem((2, 2, ROWS, HALF), f32),
        vmem((2, 2, ROWS, HALF), f32), vmem((2, 8, HALF), f32),
        vmem((2, HALF), f32), every, lines, every, every, lines, lines, every,
        vmem((OWNERS + 1, 1, HALF), f32), vmem((OWNERS, 1, HALF), f32),
        vmem((OWNERS + 1, 1, HALF), f32), vmem((OWNERS, 1, HALF), f32),
        vmem((5, 2, HALF), f32), vmem((OWNERS, 5, 2, HALF), f32),
        vmem((1, HALF), f32), vmem((DIRS - 1, 1, HALF), f32),
        vmem((ROWS, HALF), f32), vmem((HALF, HALF), f32), vmem((8, HALF), f32),
        vmem((BANDS - 1, 5, 2, HALF), f32),
        dma((2, 8)), *([dma(())] * 15), dma((DIRS - 1,)),
    ]
    smem = pl.BlockSpec(memory_space=pltpu.SMEM)
    hbm = pl.BlockSpec(memory_space=pl.ANY)
    inside = pl.BlockSpec(memory_space=pltpu.VMEM)
    delivered, coefficients, norms = pl.pallas_call(
        kernel,
        out_shape=(
            jax.ShapeDtypeStruct((2, 8, 2, 256), f32),
            jax.ShapeDtypeStruct((TERMS, 8, 2, 256), f32),
            jax.ShapeDtypeStruct((1, HALF), f32),
        ),
        in_specs=[smem, smem, hbm, hbm],
        out_specs=(inside, inside, inside),
        scratch_shapes=scratch,
        compiler_params=pltpu.CompilerParams(
            collective_id=0, has_side_effects=True, vmem_limit_bytes=48 * 1024 * 1024
        ),
        name="admm",
    )(rfi_flags, destination, visibilities, sky_model)
    return delivered, coefficients, norms[0, :4].reshape(2, 2)


def solution(mesh):
    return jax.shard_map(
        per_device,
        mesh=mesh,
        in_specs=(
            P("band", "dir", None, None, None),
            P("band", "dir", None, None, None),
            P("band", None, None),
            P("band"),
        ),
        out_specs=(P("band", "dir", None, None), P(None, "dir", None, None), P()),
        check_vma=False,
    )
```

profile of v0, /device:TPU:1, one launch (start us, length us, event | category | flops | bytes accessed | tf_op | source)
XLA Modules:
  0.0 64.9 jit_solution(13021123518837046920)
XLA Ops:
  0.6 0.0 copy-start
  0.6 2.2 %copy-done = bf16[2,8,2,256,256]{4,3,2,1,0:T(8,128)(2,1)S(1)} copy-done((bf16[2,8,2,256,256]{4,3,2,1,0:T(8,128)(2,1)S(1)}, bf16[2,8,2,256,256]{4,3,2,1,0:T(8,128)(2,1)}, u32[]{:S(2)}) %copy-start) | copy-done | bytes 4194328
  2.8 0.0 copy-start.1
  2.8 0.7 %copy-done.1 = s32[2,8,8]{2,1,0:T(8,128)S(1)} copy-done((s32[2,8,8]{2,1,0:T(8,128)S(1)}, s32[2,8,8]{2,1,0:T(8,128)}, u32[]{:S(2)}) %copy-start.1) | copy-done | bytes 536
  3.5 0.0 copy-start.2
  3.5 0.7 %copy-done.2 = s32[2]{0:T(128)S(1)} copy-done((s32[2]{0:T(128)S(1)}, s32[2]{0:T(128)}, u32[]{:S(2)}) %copy-start.2) | copy-done | bytes 32
  4.2 58.8 %admm.1 = (f32[2,8,2,256]{3,2,1,0:T(2,128)S(1)}, f32[9,8,2,256]{3,2,1,0:T(2,128)S(1)}, f32[1,128]{1,0:T(1,128)S(1)}) custom-call(s32[2,8,8]{2,1,0:T(8,128)S(1)} %copy-done.1, s32[2]{0:T(128)S(1)} %copy-done.2, bf16[2,8,2,256,256]{4,3,2,1,0:T(8,128)(2,1)S(1)} %copy-done, bf16[2,8,2,256,256]{4,3,2,1,0:T(8,128)(2,1)} %sky.1), custom_call_target="tpu_custom_call" | custom-call | tf_op jit(solution)/shard_map/admm/pallas_call | solution.py:449
  63.0 0.6 reshape_squeeze.3
  63.7 0.6 copy.9
  64.3 0.7 %copy.10 = f32[9,8,2,256]{3,2,1,0:T(2,128)} copy(f32[9,8,2,256]{3,2,1,0:T(2,128)S(1)} %get-tuple-element.13) | data formatting | bytes 294912
  (1 shorter events, 0.0 us)
Async XLA Ops:
  0.6 2.2 %copy-start = (bf16[2,8,2,256,256]{4,3,2,1,0:T(8,128)(2,1)S(1)}, bf16[2,8,2,256,256]{4,3,2,1,0:T(8,128)(2,1)}, u32[]{:S(2)}) copy-start(bf16[2,8,2,256,256]{4,3,2,1,0:T(8,128)(2,1)} %vis.1) | copy-start | bytes 12582916
  2.8 0.7 %copy-start.1 = (s32[2,8,8]{2,1,0:T(8,128)S(1)}, s32[2,8,8]{2,1,0:T(8,128)}, u32[]{:S(2)}) copy-start(s32[2,8,8]{2,1,0:T(8,128)} %flags.1) | copy-start | bytes 1540
  3.5 0.7 %copy-start.2 = (s32[2]{0:T(128)S(1)}, s32[2]{0:T(128)}, u32[]{:S(2)}) copy-start(s32[2]{0:T(128)} %dest.1) | copy-start | bytes 28
where the time goes:
time: 65.1 us; the launch traced here: 64.9 us
  Pallas kernels  58.8 us (90%)
  local copies, waits for them, and re-layouts  5.47 us (8%)
    pallas_call x1, Pallas kernels, per_device(): pl.pallas_call(kernel, out_shape=(jax.ShapeDtypeStruct((2, 8, 2, 256), f3...  58.8 us
    unnamed x8, local copies, waits for them, and re-layouts  4.81 us

commit v1 on v0

v1 whole, which is shorter than its diff:
```python
import jax
import jax.numpy as jnp
from jax import lax
from jax.experimental import pallas as pl
from jax.experimental.pallas import tpu as pltpu
from jax.sharding import PartitionSpec as P

DEGREE = 8
SWEEPS = 4
TERMS = DEGREE + 1
BANDS = 64
OWNERS = 32
DIRS = 4
ROWS = 16
HALF = 128

f32 = jnp.float32
bf16 = jnp.bfloat16
HIGHEST = lax.Precision.HIGHEST
MESH = pl.DeviceIdType.MESH
penalty_share = 0.4


def iota(shape, dim):
    return lax.broadcasted_iota(jnp.int32, shape, dim)


def gather(x, index, axis):
    return jnp.take_along_axis(x, index, axis=axis, mode="promise_in_bounds")


def dot(a, b, contract):
    return lax.dot_general(
        a, b, (contract, ((), ())), precision=HIGHEST, preferred_element_type=f32
    )


def hops(t):
    x, z = t // 8, t % 8
    return min(x, 4 - x) + min(z, 8 - z)


FAR_FIRST = sorted(range(1, OWNERS), key=lambda t: -hops(t))


def kernel(
    flags_hbm, dest_hbm, vis, sky, dlv_out, coef_out, norm_out,
    flags, dest, visb, skyb, are, aim, bsq, tc, tm, tp, tmag, num, row, tgt, pens,
    wsend, wrecv, asend, arecv, bsend, brecv, csend, crecv, near_s, far_s, near_r, far_r,
    dsend, drecv, esend, erecv, nsend, nrecv, proj, spread, norm0, dummy,
    in_sem, s_sem, w_ss, w_rs, a_ss, a_rs, b_ss, b_rs, c_ss, c_rs, n_ss, n_rs, f_ss, f_rs,
    d_ss, d_rs, e_ss, m_ss, m_rs, e_rs,
):
    me = lax.axis_index("band")
    plane = lax.axis_index("dir")
    chip = me // 2
    core = me - 2 * chip

    def wrapped(i, count):
        return jnp.where(i >= count, i - count, i)

    def copy_to(src, dst, ss, rs, target):
        return pltpu.make_async_remote_copy(
            src_ref=src, dst_ref=dst, send_sem=ss, recv_sem=rs,
            device_id={"band": target}, device_id_type=MESH,
        )

    def chunk(i, arr, buf, s):
        f, c = i // 4, lax.rem(i, 4)
        rows = pl.ds(pl.multiple_of(c * 64, 64), 64)
        return pltpu.make_async_copy(
            arr.at[f, :, :, rows, :], buf.at[f, :, :, rows, :], in_sem.at[s, i]
        )

    for i in range(8):
        chunk(i, vis, visb, 0).start()
        chunk(i, sky, skyb, 1).start()

    small = [
        pltpu.make_async_copy(flags_hbm, flags, s_sem.at[0]),
        pltpu.make_async_copy(dest_hbm, dest, s_sem.at[1]),
    ]
    for c in small:
        c.start()

    barrier = pltpu.get_barrier_semaphore()
    far = wrapped(me + BANDS // 2, BANDS)

    def greet(where):
        pl.semaphore_signal(barrier, inc=1, device_id=where, device_id_type=MESH)

    for t in FAR_FIRST:
        greet({"band": 2 * wrapped(chip + t, OWNERS) + 1})

    @pl.when(core == 0)
    def _():
        greet({"band": me + 1})
        greet({"band": far})

    @pl.when(core == 1)
    def _():
        for t in FAR_FIRST:
            greet({"band": 2 * wrapped(chip + t, OWNERS)})
        greet({"band": me - 1})
        for t in range(1, DIRS):
            greet({"dir": wrapped(plane + t, DIRS)})

    for c in small:
        c.wait()
    for f in range(2):
        count = jnp.int32(0)
        for a in range(8):
            for b in range(8):
                count = count + (1 - flags[f, a, b])
        weight = (1.0 + jnp.full((8, HALF), count, jnp.int32).astype(f32)) / 65.0
        pens[f] = penalty_share * 256.0 * weight
        wsend[pl.ds(f, 1), :] = weight[0:1, :]

    lane16 = iota((8, HALF), 1) % 16
    group = iota((8, HALF), 1) // 16
    sub = iota((8, HALF), 0)
    spread_index = [group * 16 + half * 8 + sub for half in range(2)]
    mix1 = (group + sub) % 8 * 16 + lane16
    mix2 = (sub - group + 8) % 8
    mix3 = (sub - group + 8) % 8 * 16 + lane16

    def swap_groups(x):
        return gather(gather(gather(x, mix1, 1), mix2, 0), mix3, 1)

    q_lane = iota((ROWS, HALF), 1)
    p_sub = iota((ROWS, HALF), 0)

    def operator_block(t, _):
        f, block = t // 8, t % 8

        @pl.when(block % 2 == 0)
        def _():
            chunk(t // 2, vis, visb, 0).wait()
            chunk(t // 2, sky, skyb, 1).wait()

        for qh in range(2):
            keep = [
                jnp.full((ROWS, HALF), 1 - flags[f, block, qh * 4 + b], jnp.int32)
                for b in range(4)
            ]
            kept = keep[3]
            for b in (2, 1, 0):
                kept = jnp.where(q_lane < (b + 1) * 32, keep[b], kept)
            lanes = pl.ds(qh * HALF, HALF)
            for u in range(2):
                ph = block * 2 + u
                rows = pl.ds(pl.multiple_of(ph * ROWS, ROWS), ROWS)
                apart = q_lane + qh * HALF != p_sub + ph * ROWS
                mask = jnp.where(apart, kept, 0).astype(f32).astype(bf16)[None]

                def flipped(x):
                    return x.reshape(HALF, HALF).T.astype(f32)

                mr = flipped(skyb[f, :, 0, rows, lanes] * mask)
                mi = flipped(skyb[f, :, 1, rows, lanes] * mask)
                dr = flipped(visb[f, :, 0, rows, lanes])
                di = flipped(visb[f, :, 1, rows, lanes])
                ar = mr * dr + mi * di
                ai = mr * di - mi * dr
                b2 = mr * mr + mi * mi
                are[f, ph, lanes, :] = ar
                aim[f, ph, lanes, :] = ai
                bsq[f, ph, lanes, :] = b2
                for n, v in enumerate((ar, ai, b2)):
                    part = jnp.sum(v, axis=0, keepdims=True)
                    if qh == 0:
                        num[f, n, pl.ds(ph, 1), :] = part
                    else:
                        num[f, n, pl.ds(ph, 1), :] = num[f, n, pl.ds(ph, 1), :] + part
        return 0

    lax.fori_loop(0, ROWS, operator_block, 0)

    def to_owners(src_of, dst, ss, rs):
        for t in FAR_FIRST:
            j = wrapped(chip + t, OWNERS)
            copy_to(src_of(j), dst.at[me], ss, rs, 2 * j + 1).start()

        @pl.when(core == 0)
        def _():
            copy_to(src_of(chip), dst.at[me], ss, rs, me + 1).start()

    def to_plane(src_of, dst, ss, rs):
        for t in FAR_FIRST:
            i = 2 * wrapped(chip + t, OWNERS)
            for k in range(2):
                copy_to(src_of(i + k), dst.at[chip], ss, rs, i + k).start()
        copy_to(src_of(me - 1), dst.at[chip], ss, rs, me - 1).start()

    @pl.when(core == 1)
    def _():
        wrecv[me] = wsend[...]

    ones = jnp.ones((ROWS, HALF), f32)
    zeros = jnp.zeros((ROWS, HALF), f32)
    for f in range(2):
        row[f, 0] = ones
        row[f, 1] = zeros
        tgt[f, 0] = ones
        tgt[f, 1] = zeros

    def update(f, odd):
        pen = jnp.concatenate([pens[f], pens[f]], axis=0)
        below = num[f, 2] + pen
        for part in range(2):
            fresh = (num[f, part] + pen * tgt[f, part]) / below
            row[f, part] = jnp.where(odd, 0.5 * (fresh + row[f, part]), fresh)

    def tile_row(f, r):
        for half in range(2):
            at = pl.ds(pl.multiple_of(r * ROWS + half * 8, 8), 8)
            c, d = [
                gather(
                    jnp.broadcast_to(row[f, part, pl.ds(r, 1), :], (8, HALF)),
                    spread_index[half],
                    1,
                )
                for part in range(2)
            ]
            tc[f, at, :] = c
            tm[f, at, :] = d - c
            tp[f, at, :] = d + c
            tmag[f, at, :] = c * c + d * d

    GROUP = 8

    def sweep(f, odd):
        def block(pb, _):
            acc = [[jnp.zeros((8, HALF), f32) for _ in range(4)] for _ in range(GROUP)]
            for q in range(32):
                at = pl.ds(q * 8, 8)
                c, m, p, g = tc[f, at, :], tm[f, at, :], tp[f, at, :], tmag[f, at, :]
                for j in range(GROUP):
                    ph = pb * GROUP + j
                    a, b = are[f, ph, at, :], aim[f, ph, at, :]
                    terms = ((a + b) * c, a * m, b * p, bsq[f, ph, at, :] * g)
                    acc[j] = [x + y for x, y in zip(acc[j], terms)]
            for j in range(GROUP):
                k1, k2, k3, below = acc[j]
                for n, v in enumerate((k1 - k3, k1 + k2, below)):
                    num[f, n, pl.ds(pb * GROUP + j, 1), :] = jnp.sum(v, axis=0, keepdims=True)
            for j in range(GROUP):
                tile_row(1 - f, pb * GROUP + j)
            return 0

        lax.fori_loop(0, ROWS // GROUP, block, 0)
        update(f, odd)

    for f in range(2):
        update(f, False)
    lax.fori_loop(0, ROWS, lambda r, _: (tile_row(0, r), 0)[1], 0, unroll=True)

    def sweeps(t, _):
        sweep(t % 2, t // 2 % 2 == 1)
        return 0

    lax.fori_loop(2, 4, sweeps, 0)

    pl.semaphore_wait(barrier, jnp.where(core == 1, BANDS - 1 + DIRS - 1, OWNERS + 1))
    to_owners(lambda j: wsend, wrecv, w_ss, w_rs)

    lax.fori_loop(4, 2 * SWEEPS, sweeps, 0)

    def natural(f):
        return [
            [swap_groups(row[f, part, h * 8 : h * 8 + 8, :]) for h in range(2)]
            for part in range(2)
        ]

    def pack(dst):
        for f in range(2):
            n = natural(f)
            for part in range(2):
                for h in range(2):
                    dst[pl.ds((part * 2 + h) * 8, 8), f, :] = n[part][h]

    pack(asend)
    to_owners(lambda j: asend.at[j], arecv, a_ss, a_rs)

    def along(t):
        return pltpu.make_async_remote_copy(
            src_ref=esend, dst_ref=erecv.at[t - 1], send_sem=e_ss, recv_sem=e_rs.at[t - 1],
            device_id={"dir": wrapped(plane + t, DIRS)}, device_id_type=MESH,
        )

    def both(ref):
        return jnp.concatenate([ref[:, 0, :], ref[:, 1, :]], axis=0)

    near = wrapped(me + 1, BANDS)

    def await_bytes(ref, ss, rs, sent):
        c = copy_to(ref, ref, ss, rs, near)
        c.wait_send() if sent else c.wait_recv()

    @pl.when(core == 1)
    def _():
        arecv[me] = asend[chip]
        wrecv[me] = wsend[...]
        await_bytes(wrecv.at[pl.ds(0, BANDS - 1)], w_ss, w_rs, False)
        weight = both(wrecv)
        r = iota((HALF, HALF), 0)
        lane = iota((HALF, HALF), 1)
        band_row = (r % BANDS * 2 + r // BANDS).astype(f32)
        x = (2.0 * band_row + 1.0) / 128.0 - 1.0
        basis = jnp.where(lane == 0, 1.0, jnp.where(lane == 1, x, 0.0))
        before, now = jnp.ones_like(x), x
        for c in range(2, TERMS):
            before, now = now, 2.0 * x * now - before
            basis = jnp.where(lane == c, now, basis)
        weighted = basis * weight
        gram = dot(weighted, basis, ((0,), (0,)))[:ROWS, :]
        r16, l16 = iota((ROWS, HALF), 0), iota((ROWS, HALF), 1)
        m = jnp.where((r16 >= TERMS) & (l16 == r16), 1.0, gram)
        m = jnp.where(l16 == r16 + 16, 1.0, m)
        for c in range(TERMS):
            line = m[c : c + 1, :] / m[c : c + 1, c : c + 1]
            m = jnp.where(r16 == c, line, m - m[:, c : c + 1] * line)
        inverse = m[:, 16:32]
        proj[...] = dot(inverse, weighted[:, :ROWS], ((1,), (1,)))
        spread[...] = dot(basis[:, :ROWS], proj[...], ((1,), (0,)))
        scale = 1.0 / (16384.0 * jnp.sum(weight, axis=0, keepdims=True))

        await_bytes(arecv.at[pl.ds(0, BANDS - 1)], a_ss, a_rs, False)
        gain = both(arecv)
        fresh = dot(spread[...], gain, ((1,), (0,)))
        bsend[:, 0, :] = fresh[:BANDS, :]
        bsend[:, 1, :] = fresh[BANDS:, :]

        to_plane(lambda i: bsend.at[i], brecv, b_ss, b_rs)
        brecv[chip] = bsend[me]
        first = jnp.where(chip < 16, 1.0, 0.0)
        norm0[0:1, :] = scale * jnp.sum(weight * (gain - fresh) ** 2, axis=0, keepdims=True)
        norm0[1:2, :] = scale * jnp.sum(weight * (fresh - first) ** 2, axis=0, keepdims=True)
        norm0[2:3, :] = scale
        await_bytes(brecv.at[pl.ds(0, OWNERS - 1)], b_ss, b_rs, False)

    @pl.when(core == 0)
    def _():
        await_bytes(brecv, b_ss, b_rs, False)

    for f in range(2):
        for part in range(2):
            for h in range(2):
                lines = brecv[pl.ds((part * 2 + h) * 8, 8), f, :]
                at = slice(h * 8, h * 8 + 8)
                tgt[f, part, at, :] = 2.0 * swap_groups(lines) - row[f, part, at, :]

    lax.fori_loop(0, 2 * SWEEPS, sweeps, 0)

    pack(csend)
    to_owners(lambda j: csend.at[j], crecv, c_ss, c_rs)

    first_near = jnp.full((OWNERS, HALF), dest[0] // 2, jnp.int32) == near
    row_a, row_b = csend[:, 0, :], csend[:, 1, :]
    near_rows = jnp.where(first_near, row_a, row_b)
    far_rows = jnp.where(first_near, row_b, row_a)
    near_s[pl.ds(0, OWNERS), 0, :] = near_rows
    far_s[...] = far_rows.reshape(OWNERS, 1, HALF)
    slots = [jnp.full((1, HALF), dest[f] % 2, jnp.int32).astype(f32) for f in range(2)]
    near_s[pl.ds(OWNERS, 1), 0, :] = jnp.where(first_near[:1], slots[0], slots[1])
    copy_to(near_s, near_r, n_ss, n_rs, near).start()
    copy_to(far_s, far_r, f_ss, f_rs, far).start()

    @pl.when(core == 1)
    def _():
        crecv[me] = csend[chip]
        gain0 = both(arecv)
        fresh0 = both(bsend)
        weight = both(wrecv)
        scale = norm0[2:3, :]
        await_bytes(crecv.at[pl.ds(0, BANDS - 1)], c_ss, c_rs, False)
        gain = both(crecv)
        moved = gain + (gain0 - fresh0)
        coef = dot(proj[...], moved, ((1,), (0,)))
        fresh = dot(spread[...], moved, ((1,), (0,)))
        primal = scale * jnp.sum(weight * (gain - fresh) ** 2, axis=0, keepdims=True)
        dual = scale * jnp.sum(weight * (fresh - fresh0) ** 2, axis=0, keepdims=True)
        lane = iota((1, HALF), 1)
        line = jnp.zeros((1, HALF), f32)
        for n, v in enumerate((norm0[0:1, :], norm0[1:2, :], primal, dual)):
            line = jnp.where(lane == n, jnp.sum(v, axis=1, keepdims=True), line)
        esend[...] = line
        for t in range(1, DIRS):
            along(t).start()
        for k in range(4):
            dsend[k] = coef[2 * k : 2 * k + 2, :]
        dsend[4] = coef[8:10, :]
        to_plane(lambda i: dsend, drecv, d_ss, d_rs)
        drecv[chip] = dsend[...]
        for t in range(1, DIRS):
            along(t).wait_recv()
        for t in range(1, DIRS):
            line = line + erecv[t - 1]
        nsend[...] = line
        to_plane(lambda i: nsend, nrecv, m_ss, m_rs)
        nrecv[chip] = line

    await_bytes(near_r, n_ss, n_rs, False)
    await_bytes(far_r, f_ss, f_rs, False)
    slot = near_r[OWNERS, 0:1, :]
    for part in range(2):
        for h in range(2):
            at = pl.ds((part * 2 + h) * 8, 8)
            a, b = near_r[at, 0, :], far_r[at, 0, :]
            swap = jnp.broadcast_to(slot, (8, HALF)) > 0.5
            lanes = pl.ds(h * HALF, HALF)
            dlv_out[0, :, part, lanes] = jnp.where(swap, b, a)
            dlv_out[1, :, part, lanes] = jnp.where(swap, a, b)

    @pl.when(core == 1)
    def _():
        await_bytes(drecv.at[pl.ds(0, OWNERS - 1)], d_ss, d_rs, False)

    @pl.when(core == 0)
    def _():
        await_bytes(drecv, d_ss, d_rs, False)

    for c in range(TERMS):
        for part in range(2):
            for h in range(2):
                at = pl.ds((part * 2 + h) * 8, 8)
                coef_out[c, :, part, pl.ds(h * HALF, HALF)] = drecv[at, c // 2, c % 2, :]
    @pl.when(core == 1)
    def _():
        await_bytes(nrecv.at[pl.ds(0, OWNERS - 1)], m_ss, m_rs, False)

    @pl.when(core == 0)
    def _():
        await_bytes(nrecv, m_ss, m_rs, False)

    norm = jnp.sqrt(jnp.sum(nrecv[...], axis=0))
    norm_out[...] = jnp.concatenate([norm[:, 0:2], norm[:, 2:4]], axis=0)

    await_bytes(near_s, n_ss, n_rs, True)
    await_bytes(far_s, f_ss, f_rs, True)

    @pl.when(core == 1)
    def _():
        await_bytes(wrecv.at[pl.ds(0, OWNERS - 1)], w_ss, w_rs, True)
        await_bytes(asend.at[pl.ds(0, OWNERS - 1)], a_ss, a_rs, True)
        await_bytes(csend.at[pl.ds(0, OWNERS - 1)], c_ss, c_rs, True)
        await_bytes(bsend.at[pl.ds(0, BANDS - 1)], b_ss, b_rs, True)
        await_bytes(dummy, d_ss, d_rs, True)
        await_bytes(dummy.at[:, 0, pl.ds(0, 1), :], m_ss, m_rs, True)
        await_bytes(erecv, e_ss, e_rs.at[0], True)

    @pl.when(core == 0)
    def _():
        await_bytes(wrecv.at[pl.ds(0, OWNERS)], w_ss, w_rs, True)
        await_bytes(asend, a_ss, a_rs, True)
        await_bytes(csend, c_ss, c_rs, True)


def settle(*refs):
    for i in range(3):
        refs[3 + i][...] = refs[i][...]


def per_device(visibilities, sky_model, rfi_flags, destination):
    vmem = pltpu.VMEM
    dma = pltpu.SemaphoreType.DMA
    big = vmem((2, ROWS, 256, HALF), f32)
    tile = vmem((2, 256, HALF), f32)
    lines = vmem((OWNERS, 2, HALF), f32)
    every = vmem((BANDS, 2, HALF), f32)
    scratch = [
        pltpu.SMEM((2, 8, 8), jnp.int32), pltpu.SMEM((2,), jnp.int32),
        vmem((2, 8, 2, 256, 256), bf16), vmem((2, 8, 2, 256, 256), bf16),
        big, big, big, tile, tile, tile, tile,
        vmem((2, 3, ROWS, HALF), f32), vmem((2, 2, ROWS, HALF), f32),
        vmem((2, 2, ROWS, HALF), f32), vmem((2, 8, HALF), f32),
        vmem((2, HALF), f32), every, lines, every, every, lines, lines, every,
        vmem((OWNERS + 1, 1, HALF), f32), vmem((OWNERS, 1, HALF), f32),
        vmem((OWNERS + 1, 1, HALF), f32), vmem((OWNERS, 1, HALF), f32),
        vmem((5, 2, HALF), f32), vmem((OWNERS, 5, 2, HALF), f32),
        vmem((1, HALF), f32), vmem((DIRS - 1, 1, HALF), f32),
        vmem((1, HALF), f32), vmem((OWNERS, 1, HALF), f32),
        vmem((ROWS, HALF), f32), vmem((HALF, HALF), f32), vmem((8, HALF), f32),
        vmem((BANDS - 1, 5, 2, HALF), f32),
        dma((2, 8)), dma((2,)), *([dma(())] * 17), dma((DIRS - 1,)),
    ]
    hbm = pl.BlockSpec(memory_space=pl.ANY)
    inside = pl.BlockSpec(memory_space=pltpu.VMEM)
    results = pl.pallas_call(
        kernel,
        out_shape=(
            jax.ShapeDtypeStruct((2, 8, 2, 256), f32),
            jax.ShapeDtypeStruct((TERMS, 8, 2, 256), f32),
            jax.ShapeDtypeStruct((2, 2), f32),
        ),
        in_specs=[hbm] * 4,
        out_specs=(inside, inside, inside),
        scratch_shapes=scratch,
        compiler_params=pltpu.CompilerParams(
            collective_id=0, has_side_effects=True, vmem_limit_bytes=62 * 1024 * 1024
        ),
        name="admm",
    )(rfi_flags, destination, visibilities, sky_model)
    return pl.pallas_call(
        settle,
        out_shape=tuple(jax.ShapeDtypeStruct(r.shape, r.dtype) for r in results),
        name="settle",
    )(*results)


def solution(mesh):
    return jax.shard_map(
        per_device,
        mesh=mesh,
        in_specs=(
            P("band", "dir", None, None, None),
            P("band", "dir", None, None, None),
            P("band", None, None),
            P("band"),
        ),
        out_specs=(P("band", "dir", None, None), P(None, "dir", None, None), P()),
        check_vma=False,
    )
```

time: 65.1 us -> 52.1 us (0.80)
  Pallas kernels: 58.8 us -> 51.4 us
  local copies, waits for them, and re-layouts: 5.47 us -> 0 us
    pallas_call x1, Pallas kernels: 58.8 us -> 49.8 us  [per_device(): pl.pallas_call(kernel, out_shape=(jax.ShapeDtypeStruct((2, 8, 2, 256), f3...]
    unnamed x8 -> x0, local copies, waits for them, and re-layouts: 4.81 us -> none
    pallas_call x0 -> x1, Pallas kernels: none -> 1.59 us  [per_device(): pl.pallas_call(settle, out_shape=tuple((jax.ShapeDtypeStruct(r.shape, r.d...]
where the time goes in v1:
time: 52.1 us; the launch traced here: 52 us
  Pallas kernels  51.4 us (99%)
  between operations  0.64 us (1%)
    pallas_call x1, Pallas kernels, per_device(): pl.pallas_call(kernel, out_shape=(jax.ShapeDtypeStruct((2, 8, 2, 256), f3...  49.8 us
    pallas_call x1, Pallas kernels, per_device(): pl.pallas_call(settle, out_shape=tuple((jax.ShapeDtypeStruct(r.shape, r.d...  1.59 us

profile of v1, /device:TPU:1, one launch (start us, length us, event | category | flops | bytes accessed | tf_op | source)
XLA Modules:
  0.0 52.0 jit_solution(14816693931757752614)
XLA Ops:
  0.6 49.8 %admm.1 = (f32[2,8,2,256]{3,2,1,0:T(2,128)}, f32[9,8,2,256]{3,2,1,0:T(2,128)}, f32[2,2]{1,0:T(2,128)}) custom-call(s32[2,8,8]{2,1,0:T(8,128)} %flags_hbm.1, s32[2]{0:T(128)} %dest_hbm.1, bf16[2,8,2,256,256]{4,3,2,1,0:T(8,128)(2,1)} %vis.1, bf16[2,8,2,256,256]{4,3,2,1,0:T(8,128)(2,1)} %sky.1), custom_call_target="tpu_custom_call" | custom-call | tf_op jit(solution)/shard_map/admm/pallas_call | solution.py:489
  50.4 1.6 %settle.1 = (f32[2,8,2,256]{3,2,1,0:T(2,128)}, f32[9,8,2,256]{3,2,1,0:T(2,128)}, f32[2,2]{1,0:T(2,128)}) custom-call(f32[2,8,2,256]{3,2,1,0:T(2,128)} %get-tuple-element.6.refs_0_, f32[9,8,2,256]{3,2,1,0:T(2,128)} %get-tuple-element.7.refs_1_, f32[2,2]{1,0:T(2,128)} %get-tuple-element.8.refs_2_), custom_call_target="tpu_custom_call" | custom-call | tf_op jit(solution)/shard_map/settle/pallas_call | solution.py:504

commit v2 on v1

--- a/solution.py
+++ b/solution.py
@@ -41,6 +41,10 @@
 
 
 FAR_FIRST = sorted(range(1, OWNERS), key=lambda t: -hops(t))
+SERVED = sorted(
+    ((dx, dz) for dx in range(4) for dz in range(-2, 2) if (dx, dz) != (0, 0)),
+    key=lambda d: -(min(d[0], 4 - d[0]) + abs(d[1])),
+)
 
 
 def kernel(
@@ -58,6 +62,9 @@
 
     def wrapped(i, count):
         return jnp.where(i >= count, i - count, i)
+
+    x, z = chip // 8, chip % 8
+    columns = 2 * (4 * x + wrapped(z, 4))
 
     def copy_to(src, dst, ss, rs, target):
         return pltpu.make_async_remote_copy(
@@ -176,25 +183,26 @@
 
     lax.fori_loop(0, ROWS, operator_block, 0)
 
-    def to_owners(src_of, dst, ss, rs):
+    def to_owners(src, dst, ss, rs, shared=False):
+        def part(c):
+            if shared:
+                return src
+            return src.at[pl.ds(2 * (4 * (c // 8) + wrapped(c % 8, 4)), 2)]
+
         for t in FAR_FIRST:
-            j = wrapped(chip + t, OWNERS)
-            copy_to(src_of(j), dst.at[me], ss, rs, 2 * j + 1).start()
+            c = wrapped(chip + t, OWNERS)
+            copy_to(part(c), dst.at[me], ss, rs, 2 * c + 1).start()
 
         @pl.when(core == 0)
         def _():
-            copy_to(src_of(chip), dst.at[me], ss, rs, me + 1).start()
-
-    def to_plane(src_of, dst, ss, rs):
-        for t in FAR_FIRST:
-            i = 2 * wrapped(chip + t, OWNERS)
+            copy_to(part(chip), dst.at[me], ss, rs, me + 1).start()
+
+    def to_served(src_of, dst, ss, rs):
+        for dx, dz in SERVED:
+            i = 2 * (8 * wrapped(x + dx, 4) + wrapped(z + dz % 8, 8))
             for k in range(2):
-                copy_to(src_of(i + k), dst.at[chip], ss, rs, i + k).start()
-        copy_to(src_of(me - 1), dst.at[chip], ss, rs, me - 1).start()
-
-    @pl.when(core == 1)
-    def _():
-        wrecv[me] = wsend[...]
+                copy_to(src_of(i + k), dst, ss, rs, i + k).start()
+        copy_to(src_of(me - 1), dst, ss, rs, me - 1).start()
 
     ones = jnp.ones((ROWS, HALF), f32)
     zeros = jnp.zeros((ROWS, HALF), f32)
@@ -262,7 +270,7 @@
     lax.fori_loop(2, 4, sweeps, 0)
 
     pl.semaphore_wait(barrier, jnp.where(core == 1, BANDS - 1 + DIRS - 1, OWNERS + 1))
-    to_owners(lambda j: wsend, wrecv, w_ss, w_rs)
+    to_owners(wsend, wrecv, w_ss, w_rs, shared=True)
 
     lax.fori_loop(4, 2 * SWEEPS, sweeps, 0)
 
@@ -280,7 +288,11 @@
                     dst[pl.ds((part * 2 + h) * 8, 8), f, :] = n[part][h]
 
     pack(asend)
-    to_owners(lambda j: asend.at[j], arecv, a_ss, a_rs)
+    to_owners(asend, arecv, a_ss, a_rs)
+
+    def folded(v):
+        v = jnp.sum(v, axis=0, keepdims=True)
+        return v[:, :HALF] + v[:, HALF:]
 
     def along(t):
         return pltpu.make_async_remote_copy(
@@ -291,6 +303,11 @@
     def both(ref):
         return jnp.concatenate([ref[:, 0, :], ref[:, 1, :]], axis=0)
 
+    mine = pl.ds(columns, 2)
+
+    def chunks(ref):
+        return jnp.concatenate([both(ref.at[:, k]) for k in range(2)], axis=1)
+
     near = wrapped(me + 1, BANDS)
 
     def await_bytes(ref, ss, rs, sent):
@@ -299,18 +316,19 @@
 
     @pl.when(core == 1)
     def _():
-        arecv[me] = asend[chip]
+        arecv[me] = asend[mine]
         wrecv[me] = wsend[...]
         await_bytes(wrecv.at[pl.ds(0, BANDS - 1)], w_ss, w_rs, False)
         weight = both(wrecv)
+        wide = jnp.concatenate([weight, weight], axis=1)
         r = iota((HALF, HALF), 0)
         lane = iota((HALF, HALF), 1)
         band_row = (r % BANDS * 2 + r // BANDS).astype(f32)
-        x = (2.0 * band_row + 1.0) / 128.0 - 1.0
-        basis = jnp.where(lane == 0, 1.0, jnp.where(lane == 1, x, 0.0))
-        before, now = jnp.ones_like(x), x
+        u = (2.0 * band_row + 1.0) / 128.0 - 1.0
+        basis = jnp.where(lane == 0, 1.0, jnp.where(lane == 1, u, 0.0))
+        before, now = jnp.ones_like(u), u
         for c in range(2, TERMS):
-            before, now = now, 2.0 * x * now - before
+            before, now = now, 2.0 * u * now - before
             basis = jnp.where(lane == c, now, basis)
         weighted = basis * weight
         gram = dot(weighted, basis, ((0,), (0,)))[:ROWS, :]
@@ -326,18 +344,19 @@
         scale = 1.0 / (16384.0 * jnp.sum(weight, axis=0, keepdims=True))
 
         await_bytes(arecv.at[pl.ds(0, BANDS - 1)], a_ss, a_rs, False)
-        gain = both(arecv)
+        gain = chunks(arecv)
         fresh = dot(spread[...], gain, ((1,), (0,)))
-        bsend[:, 0, :] = fresh[:BANDS, :]
-        bsend[:, 1, :] = fresh[BANDS:, :]
-
-        to_plane(lambda i: bsend.at[i], brecv, b_ss, b_rs)
-        brecv[chip] = bsend[me]
-        first = jnp.where(chip < 16, 1.0, 0.0)
-        norm0[0:1, :] = scale * jnp.sum(weight * (gain - fresh) ** 2, axis=0, keepdims=True)
-        norm0[1:2, :] = scale * jnp.sum(weight * (fresh - first) ** 2, axis=0, keepdims=True)
+        for k in range(2):
+            lanes = slice(k * HALF, (k + 1) * HALF)
+            for f in range(2):
+                bsend[:, k, f, :] = fresh[f * BANDS : (f + 1) * BANDS, lanes]
+        to_served(lambda i: bsend.at[i], brecv.at[mine], b_ss, b_rs)
+        brecv[mine] = bsend[me]
+        first = jnp.where(x < 2, 1.0, 0.0)
+        norm0[0:1, :] = folded(wide * (gain - fresh) ** 2)
+        norm0[1:2, :] = folded(wide * (fresh - first) ** 2)
         norm0[2:3, :] = scale
-        await_bytes(brecv.at[pl.ds(0, OWNERS - 1)], b_ss, b_rs, False)
+        await_bytes(brecv.at[pl.ds(0, OWNERS - 2)], b_ss, b_rs, False)
 
     @pl.when(core == 0)
     def _():
@@ -353,7 +372,7 @@
     lax.fori_loop(0, 2 * SWEEPS, sweeps, 0)
 
     pack(csend)
-    to_owners(lambda j: csend.at[j], crecv, c_ss, c_rs)
+    to_owners(csend, crecv, c_ss, c_rs)
 
     first_near = jnp.full((OWNERS, HALF), dest[0] // 2, jnp.int32) == near
     row_a, row_b = csend[:, 0, :], csend[:, 1, :]
@@ -368,37 +387,40 @@
 
     @pl.when(core == 1)
     def _():
-        crecv[me] = csend[chip]
-        gain0 = both(arecv)
-        fresh0 = both(bsend)
+        crecv[me] = csend[mine]
+        gain0 = chunks(arecv)
+        fresh0 = chunks(bsend)
         weight = both(wrecv)
+        wide = jnp.concatenate([weight, weight], axis=1)
         scale = norm0[2:3, :]
         await_bytes(crecv.at[pl.ds(0, BANDS - 1)], c_ss, c_rs, False)
-        gain = both(crecv)
+        gain = chunks(crecv)
         moved = gain + (gain0 - fresh0)
         coef = dot(proj[...], moved, ((1,), (0,)))
         fresh = dot(spread[...], moved, ((1,), (0,)))
-        primal = scale * jnp.sum(weight * (gain - fresh) ** 2, axis=0, keepdims=True)
-        dual = scale * jnp.sum(weight * (fresh - fresh0) ** 2, axis=0, keepdims=True)
+        primal = folded(wide * (gain - fresh) ** 2)
+        dual = folded(wide * (fresh - fresh0) ** 2)
         lane = iota((1, HALF), 1)
         line = jnp.zeros((1, HALF), f32)
         for n, v in enumerate((norm0[0:1, :], norm0[1:2, :], primal, dual)):
-            line = jnp.where(lane == n, jnp.sum(v, axis=1, keepdims=True), line)
+            line = jnp.where(lane == n, jnp.sum(scale * v, axis=1, keepdims=True), line)
         esend[...] = line
         for t in range(1, DIRS):
             along(t).start()
-        for k in range(4):
-            dsend[k] = coef[2 * k : 2 * k + 2, :]
-        dsend[4] = coef[8:10, :]
-        to_plane(lambda i: dsend, drecv, d_ss, d_rs)
-        drecv[chip] = dsend[...]
+        for k in range(2):
+            lanes = slice(k * HALF, (k + 1) * HALF)
+            for n in range(5):
+                dsend[k, n] = coef[2 * n : 2 * n + 2, lanes]
+        to_served(lambda i: dsend, drecv.at[mine], d_ss, d_rs)
+        drecv[mine] = dsend[...]
         for t in range(1, DIRS):
             along(t).wait_recv()
         for t in range(1, DIRS):
             line = line + erecv[t - 1]
         nsend[...] = line
-        to_plane(lambda i: nsend, nrecv, m_ss, m_rs)
-        nrecv[chip] = line
+        group = columns // 2
+        to_served(lambda i: nsend, nrecv.at[group], m_ss, m_rs)
+        nrecv[group] = line
 
     await_bytes(near_r, n_ss, n_rs, False)
     await_bytes(far_r, f_ss, f_rs, False)
@@ -414,7 +436,7 @@
 
     @pl.when(core == 1)
     def _():
-        await_bytes(drecv.at[pl.ds(0, OWNERS - 1)], d_ss, d_rs, False)
+        await_bytes(drecv.at[pl.ds(0, OWNERS - 2)], d_ss, d_rs, False)
 
     @pl.when(core == 0)
     def _():
@@ -427,7 +449,7 @@
                 coef_out[c, :, part, pl.ds(h * HALF, HALF)] = drecv[at, c // 2, c % 2, :]
     @pl.when(core == 1)
     def _():
-        await_bytes(nrecv.at[pl.ds(0, OWNERS - 1)], m_ss, m_rs, False)
+        await_bytes(nrecv.at[pl.ds(0, OWNERS // 2 - 1)], m_ss, m_rs, False)
 
     @pl.when(core == 0)
     def _():
@@ -442,18 +464,18 @@
     @pl.when(core == 1)
     def _():
         await_bytes(wrecv.at[pl.ds(0, OWNERS - 1)], w_ss, w_rs, True)
-        await_bytes(asend.at[pl.ds(0, OWNERS - 1)], a_ss, a_rs, True)
-        await_bytes(csend.at[pl.ds(0, OWNERS - 1)], c_ss, c_rs, True)
-        await_bytes(bsend.at[pl.ds(0, BANDS - 1)], b_ss, b_rs, True)
+        await_bytes(arecv.at[pl.ds(0, OWNERS - 1)], a_ss, a_rs, True)
+        await_bytes(crecv.at[pl.ds(0, OWNERS - 1)], c_ss, c_rs, True)
+        await_bytes(bsend.at[pl.ds(0, OWNERS - 1)], b_ss, b_rs, True)
         await_bytes(dummy, d_ss, d_rs, True)
-        await_bytes(dummy.at[:, 0, pl.ds(0, 1), :], m_ss, m_rs, True)
+        await_bytes(dummy.at[:, 0, 0, pl.ds(0, 1), :], m_ss, m_rs, True)
         await_bytes(erecv, e_ss, e_rs.at[0], True)
 
     @pl.when(core == 0)
     def _():
         await_bytes(wrecv.at[pl.ds(0, OWNERS)], w_ss, w_rs, True)
-        await_bytes(asend, a_ss, a_rs, True)
-        await_bytes(csend, c_ss, c_rs, True)
+        await_bytes(arecv.at[pl.ds(0, OWNERS)], a_ss, a_rs, True)
+        await_bytes(crecv.at[pl.ds(0, OWNERS)], c_ss, c_rs, True)
 
 
 def settle(*refs):
@@ -468,20 +490,21 @@
     tile = vmem((2, 256, HALF), f32)
     lines = vmem((OWNERS, 2, HALF), f32)
     every = vmem((BANDS, 2, HALF), f32)
+    pairs = vmem((BANDS, 2, 2, HALF), f32)
     scratch = [
         pltpu.SMEM((2, 8, 8), jnp.int32), pltpu.SMEM((2,), jnp.int32),
         vmem((2, 8, 2, 256, 256), bf16), vmem((2, 8, 2, 256, 256), bf16),
         big, big, big, tile, tile, tile, tile,
         vmem((2, 3, ROWS, HALF), f32), vmem((2, 2, ROWS, HALF), f32),
         vmem((2, 2, ROWS, HALF), f32), vmem((2, 8, HALF), f32),
-        vmem((2, HALF), f32), every, lines, every, every, lines, lines, every,
+        vmem((2, HALF), f32), every, lines, pairs, pairs, lines, lines, pairs,
         vmem((OWNERS + 1, 1, HALF), f32), vmem((OWNERS, 1, HALF), f32),
         vmem((OWNERS + 1, 1, HALF), f32), vmem((OWNERS, 1, HALF), f32),
-        vmem((5, 2, HALF), f32), vmem((OWNERS, 5, 2, HALF), f32),
+        vmem((2, 5, 2, HALF), f32), vmem((OWNERS, 5, 2, HALF), f32),
         vmem((1, HALF), f32), vmem((DIRS - 1, 1, HALF), f32),
-        vmem((1, HALF), f32), vmem((OWNERS, 1, HALF), f32),
+        vmem((1, HALF), f32), vmem((OWNERS // 2, 1, HALF), f32),
         vmem((ROWS, HALF), f32), vmem((HALF, HALF), f32), vmem((8, HALF), f32),
-        vmem((BANDS - 1, 5, 2, HALF), f32),
+        vmem((OWNERS - 1, 2, 5, 2, HALF), f32),
         dma((2, 8)), dma((2,)), *([dma(())] * 17), dma((DIRS - 1,)),
     ]
     hbm = pl.BlockSpec(memory_space=pl.ANY)
@@ -489,9 +512,9 @@
     results = pl.pallas_call(
         kernel,
         out_shape=(
-            jax.ShapeDtypeStruct((2, 8, 2, 256), f32),
-            jax.ShapeDtypeStruct((TERMS, 8, 2, 256), f32),
-            jax.ShapeDtypeStruct((2, 2), f32),
+            pltpu.VMEM((2, 8, 2, 256), f32),
+            pltpu.VMEM((TERMS, 8, 2, 256), f32),
+            pltpu.VMEM((2, 2), f32),
         ),
         in_specs=[hbm] * 4,
         out_specs=(inside, inside, inside),
@@ -504,6 +527,9 @@
     return pl.pallas_call(
         settle,
         out_shape=tuple(jax.ShapeDtypeStruct(r.shape, r.dtype) for r in results),
+        in_specs=[inside] * 3,
+        out_specs=(inside,) * 3,
+        compiler_params=pltpu.CompilerParams(vmem_limit_bytes=4 * 1024 * 1024),
         name="settle",
     )(*results)
 

time: 52.1 us -> 49.1 us (0.942)
  Pallas kernels: 51.4 us -> 48.4 us
    pallas_call x1, Pallas kernels: 49.8 us -> 47.7 us  [per_device(): pl.pallas_call(kernel, out_shape=(pltpu.VMEM((2, 8, 2, 256), f32), pltpu....]
    pallas_call x1, Pallas kernels: 1.59 us -> 0.68 us  [per_device(): pl.pallas_call(settle, out_shape=tuple((jax.ShapeDtypeStruct(r.shape, r.d...]
where the time goes in v2:
time: 49.1 us; the launch traced here: 49 us
  Pallas kernels  48.4 us (99%)
  between operations  0.64 us (1%)
    pallas_call x1, Pallas kernels, per_device(): pl.pallas_call(kernel, out_shape=(pltpu.VMEM((2, 8, 2, 256), f32), pltpu....  47.7 us

profile of v2, /device:TPU:1, one launch (start us, length us, event | category | flops | bytes accessed | tf_op | source)
XLA Modules:
  0.0 49.0 jit_solution(1092847540686018008)
XLA Ops:
  0.6 47.7 %admm.1 = (f32[2,8,2,256]{3,2,1,0:T(2,128)S(1)}, f32[9,8,2,256]{3,2,1,0:T(2,128)S(1)}, f32[2,2]{1,0:T(2,128)S(1)}) custom-call(s32[2,8,8]{2,1,0:T(8,128)} %flags_hbm.1, s32[2]{0:T(128)} %dest_hbm.1, bf16[2,8,2,256,256]{4,3,2,1,0:T(8,128)(2,1)} %vis.1, bf16[2,8,2,256,256]{4,3,2,1,0:T(8,128)(2,1)} %sky.1), custom_call_target="tpu_custom_call" | custom-call | tf_op jit(solution)/shard_map/admm/pallas_call | solution.py:512
  48.4 0.7 %settle.1 = (f32[2,8,2,256]{3,2,1,0:T(2,128)}, f32[9,8,2,256]{3,2,1,0:T(2,128)}, f32[2,2]{1,0:T(2,128)}) custom-call(f32[2,8,2,256]{3,2,1,0:T(2,128)S(1)} %get-tuple-element.6.refs_0_, f32[9,8,2,256]{3,2,1,0:T(2,128)S(1)} %get-tuple-element.7.refs_1_, f32[2,2]{1,0:T(2,128)S(1)} %get-tuple-element.8.refs_2_), custom_call_target="tpu_custom_call" | custom-call | tf_op jit(solution)/shard_map/settle/pallas_call | solution.py:527

commit v3 on v2

--- a/solution.py
+++ b/solution.py
@@ -79,16 +79,15 @@
             arr.at[f, :, :, rows, :], buf.at[f, :, :, rows, :], in_sem.at[s, i]
         )
 
-    for i in range(8):
-        chunk(i, vis, visb, 0).start()
-        chunk(i, sky, skyb, 1).start()
-
     small = [
         pltpu.make_async_copy(flags_hbm, flags, s_sem.at[0]),
         pltpu.make_async_copy(dest_hbm, dest, s_sem.at[1]),
     ]
     for c in small:
         c.start()
+    for i in range(8):
+        chunk(i, vis, visb, 0).start()
+        chunk(i, sky, skyb, 1).start()
 
     barrier = pltpu.get_barrier_semaphore()
     far = wrapped(me + BANDS // 2, BANDS)
@@ -138,14 +137,12 @@
     p_sub = iota((ROWS, HALF), 0)
 
     def operator_block(t, _):
-        f, block = t // 8, t % 8
-
-        @pl.when(block % 2 == 0)
-        def _():
-            chunk(t // 2, vis, visb, 0).wait()
-            chunk(t // 2, sky, skyb, 1).wait()
-
-        for qh in range(2):
+        f, four = t // 4, t % 4
+        chunk(t, vis, visb, 0).wait()
+        chunk(t, sky, skyb, 1).wait()
+
+        for half, qh in [(half, qh) for half in range(2) for qh in range(2)]:
+            block = four * 2 + half
             keep = [
                 jnp.full((ROWS, HALF), 1 - flags[f, block, qh * 4 + b], jnp.int32)
                 for b in range(4)
@@ -181,7 +178,7 @@
                         num[f, n, pl.ds(ph, 1), :] = num[f, n, pl.ds(ph, 1), :] + part
         return 0
 
-    lax.fori_loop(0, ROWS, operator_block, 0)
+    lax.fori_loop(0, ROWS // 2, operator_block, 0)
 
     def to_owners(src, dst, ss, rs, shared=False):
         def part(c):
@@ -240,10 +237,10 @@
     def sweep(f, odd):
         def block(pb, _):
             acc = [[jnp.zeros((8, HALF), f32) for _ in range(4)] for _ in range(GROUP)]
-            for q in range(32):
+            for first, q in [(first, q) for first in (0, GROUP // 2) for q in range(32)]:
                 at = pl.ds(q * 8, 8)
                 c, m, p, g = tc[f, at, :], tm[f, at, :], tp[f, at, :], tmag[f, at, :]
-                for j in range(GROUP):
+                for j in range(first, first + GROUP // 2):
                     ph = pb * GROUP + j
                     a, b = are[f, ph, at, :], aim[f, ph, at, :]
                     terms = ((a + b) * c, a * m, b * p, bsq[f, ph, at, :] * g)

time: 49.1 us -> 47.4 us (0.965)
  Pallas kernels: 48.4 us -> 46.6 us
    pallas_call x1, Pallas kernels: 47.7 us -> 46 us  [per_device(): pl.pallas_call(kernel, out_shape=(pltpu.VMEM((2, 8, 2, 256), f32), pltpu....]
where the time goes in v3:
time: 47.4 us; the launch traced here: 47.3 us
  Pallas kernels  46.6 us (98%)
  between operations  0.64 us (1%)
    pallas_call x1, Pallas kernels, per_device(): pl.pallas_call(kernel, out_shape=(pltpu.VMEM((2, 8, 2, 256), f32), pltpu....  46 us

profile of v3, /device:TPU:1, one launch (start us, length us, event | category | flops | bytes accessed | tf_op | source)
XLA Modules:
  0.0 47.3 jit_solution(2074628863728370851)
XLA Ops:
  0.6 46.0 %admm.1 = (f32[2,8,2,256]{3,2,1,0:T(2,128)S(1)}, f32[9,8,2,256]{3,2,1,0:T(2,128)S(1)}, f32[2,2]{1,0:T(2,128)S(1)}) custom-call(s32[2,8,8]{2,1,0:T(8,128)} %flags_hbm.1, s32[2]{0:T(128)} %dest_hbm.1, bf16[2,8,2,256,256]{4,3,2,1,0:T(8,128)(2,1)} %vis.1, bf16[2,8,2,256,256]{4,3,2,1,0:T(8,128)(2,1)} %sky.1), custom_call_target="tpu_custom_call" | custom-call | tf_op jit(solution)/shard_map/admm/pallas_call | solution.py:509
  46.6 0.7 %settle.1 = (f32[2,8,2,256]{3,2,1,0:T(2,128)}, f32[9,8,2,256]{3,2,1,0:T(2,128)}, f32[2,2]{1,0:T(2,128)}) custom-call(f32[2,8,2,256]{3,2,1,0:T(2,128)S(1)} %get-tuple-element.6.refs_0_, f32[9,8,2,256]{3,2,1,0:T(2,128)S(1)} %get-tuple-element.7.refs_1_, f32[2,2]{1,0:T(2,128)S(1)} %get-tuple-element.8.refs_2_), custom_call_target="tpu_custom_call" | custom-call | tf_op jit(solution)/shard_map/settle/pallas_call | solution.py:524

commit v4 on v3

--- a/solution.py
+++ b/solution.py
@@ -393,7 +393,6 @@
         await_bytes(crecv.at[pl.ds(0, BANDS - 1)], c_ss, c_rs, False)
         gain = chunks(crecv)
         moved = gain + (gain0 - fresh0)
-        coef = dot(proj[...], moved, ((1,), (0,)))
         fresh = dot(spread[...], moved, ((1,), (0,)))
         primal = folded(wide * (gain - fresh) ** 2)
         dual = folded(wide * (fresh - fresh0) ** 2)
@@ -404,6 +403,7 @@
         esend[...] = line
         for t in range(1, DIRS):
             along(t).start()
+        coef = dot(proj[...], moved, ((1,), (0,)))
         for k in range(2):
             lanes = slice(k * HALF, (k + 1) * HALF)
             for n in range(5):

time: 47.4 us -> 47.4 us (level)
  no operation moved by 1% of the time
where the time goes in v4:
time: 47.4 us; the launch traced here: 47.3 us
  Pallas kernels  46.6 us (98%)
  between operations  0.64 us (1%)
    pallas_call x1, Pallas kernels, per_device(): pl.pallas_call(kernel, out_shape=(pltpu.VMEM((2, 8, 2, 256), f32), pltpu....  46 us

profile of v4, /device:TPU:1, one launch (start us, length us, event | category | flops | bytes accessed | tf_op | source)
XLA Modules:
  0.0 47.3 jit_solution(553820006566022396)
XLA Ops:
  0.6 46.0 %admm.1 = (f32[2,8,2,256]{3,2,1,0:T(2,128)S(1)}, f32[9,8,2,256]{3,2,1,0:T(2,128)S(1)}, f32[2,2]{1,0:T(2,128)S(1)}) custom-call(s32[2,8,8]{2,1,0:T(8,128)} %flags_hbm.1, s32[2]{0:T(128)} %dest_hbm.1, bf16[2,8,2,256,256]{4,3,2,1,0:T(8,128)(2,1)} %vis.1, bf16[2,8,2,256,256]{4,3,2,1,0:T(8,128)(2,1)} %sky.1), custom_call_target="tpu_custom_call" | custom-call | tf_op jit(solution)/shard_map/admm/pallas_call | solution.py:509
  46.6 0.7 %settle.1 = (f32[2,8,2,256]{3,2,1,0:T(2,128)}, f32[9,8,2,256]{3,2,1,0:T(2,128)}, f32[2,2]{1,0:T(2,128)}) custom-call(f32[2,8,2,256]{3,2,1,0:T(2,128)S(1)} %get-tuple-element.6.refs_0_, f32[9,8,2,256]{3,2,1,0:T(2,128)S(1)} %get-tuple-element.7.refs_1_, f32[2,2]{1,0:T(2,128)S(1)} %get-tuple-element.8.refs_2_), custom_call_target="tpu_custom_call" | custom-call | tf_op jit(solution)/shard_map/settle/pallas_call | solution.py:524
